TPU v7x, 32 devices: a whole 2x2x4 slice. The times are simulated.
32 devices in a mesh: narrow: 4 (over x, core), wide: 8 (over z, y).
Axes of the slice: x: 2, y: 2, z: 4, core: 2. Of those that a mesh axis runs over, the one named last changes fastest.
Arguments:
- block_ids: int32 [512, 4], P(('narrow', 'wide')), may hold values from 0 to 511, as said below
- incidence: int32 [512, 4, 128, 128], P(('narrow', 'wide')), may hold values from 0 to 1
- costs: int32 [512, 128], P(('narrow', 'wide')), may hold values from 16 to 80
- start_mult: float32 [512, 128], replicated, may hold values from 0.25 to 4
- upper: float32 [1], replicated, may hold values from 65536 to 131072
Outputs:
- multipliers: float32 [512, 128], replicated
- primal_mean: float32 [512, 128], P(('narrow', 'wide'))
Inputs may be any that keep to these rules, and one draw needn't show every extreme that they name: `block_ids`: the 4 row blocks listed for one tile are distinct.
All inputs are finite; a program needn't handle non-finite values.
Results may differ from a plain program's by a relative error of at most 0.0003.
Values sent between devices are 32-bit elements; how exact they have to be, the bound alone decides.
A program may use at most 64 MiB of HBM per device.

v0:
```python
import jax
import jax.numpy as jnp
from jax import lax
from jax.sharding import PartitionSpec as P

BLK = 128
K = 4
ITERS = 3


def local(block_ids, incidence, costs, start_mult, upper):
    hi = lax.Precision.HIGHEST
    tiles_here = block_ids.shape[0]
    blocks = start_mult.shape[0]
    incf = incidence.astype(jnp.float32)
    costf = costs.astype(jnp.float32)
    onehot = (
        block_ids.reshape(tiles_here * K, 1) == jnp.arange(blocks, dtype=jnp.int32)[None, :]
    ).astype(jnp.float32)
    count_narrow = lax.axis_size("narrow")
    count_wide = lax.axis_size("wide")
    share_rows = blocks // lax.axis_size(("narrow", "wide"))
    share_start = lax.axis_index(("narrow", "wide")) * share_rows
    mult = start_mult
    primal_mean = jnp.zeros(costs.shape, jnp.float32)
    for step in range(ITERS):
        u_tile = jnp.take(mult, block_ids, axis=0)
        reduced = costf - jnp.einsum("tkrc,tkr->tc", incf, u_tile, precision=hi)
        primal = 1.0 / (1.0 + jnp.exp(reduced / 8.0))
        local_soft = jnp.sum(-8.0 * jax.nn.softplus(-reduced / 8.0))
        if step == 0:
            primal_mean = primal
        else:
            primal_mean = 0.3 * primal + 0.7 * primal_mean
        part = jnp.einsum("tkrc,tc->tkr", incf, primal_mean, precision=hi).reshape(
            tiles_here * K, BLK
        )
        row_part = jnp.dot(onehot.T, part, precision=hi, preferred_element_type=jnp.float32)
        outgoing = row_part.reshape(count_narrow, count_wide, share_rows, BLK)
        incoming = lax.all_to_all(
            lax.all_to_all(outgoing, "narrow", split_axis=0, concat_axis=0, tiled=True),
            "wide",
            split_axis=1,
            concat_axis=1,
            tiled=True,
        )
        cover_share = jnp.sum(jnp.sum(incoming, axis=0), axis=0)
        mult_share = lax.dynamic_slice_in_dim(mult, share_start, share_rows, 0)
        slope = 1.0 - cover_share
        norm, mult_total, late_sum = lax.psum(
            (jnp.sum(slope * slope), jnp.sum(mult_share), local_soft), ("narrow", "wide")
        )
        value = mult_total + late_sum
        size = (upper[0] - value) / (norm + 1e-06)
        new_share = jnp.maximum(0.0, mult_share + size * slope)
        mult = lax.all_gather(new_share, ("narrow", "wide"), axis=0, tiled=True)
    return (mult, primal_mean)


def solution(mesh):
    in_specs = (
        P(("narrow", "wide"), None),
        P(("narrow", "wide"), None, None, None),
        P(("narrow", "wide"), None),
        P(),
        P(),
    )
    out_specs = (P(), P(("narrow", "wide"), None))
    return jax.shard_map(local, mesh=mesh, in_specs=in_specs, out_specs=out_specs, check_vma=False)
```

profile of v0, /device:TPU:0, one launch (start us, length us, event | category | flops | bytes accessed | tf_op | source)
XLA Modules:
  0.0 426.2 jit_solution(1178383881923371404)
XLA Ops:
  0.6 0.0 copy-start.3
  0.6 0.7 compare_and_fusion
  1.3 0.7 compare_select_fusion.3
  2.0 0.8 copy.23
  2.8 0.1 copy.21
  2.9 0.1 copy.22
  3.0 0.1 reshape.82
  3.1 0.1 eq.41
  3.2 1.5 gather_fusion
  4.7 0.0 copy-start
  4.7 0.1 broadcast_select_fusion.2
  4.8 4.1 fusion.10
  8.9 0.0 copy-done.3
  8.9 0.6 fusion.25
  9.6 0.0 copy-done
  9.6 3.4 fusion.8
  12.9 0.3 fusion.16
  13.3 10.0 %all_to_all.30 = f32[4,8,16,128]{3,2,1,0:T(8,128)S(1)} all-to-all(f32[4,8,16,128]{3,2,1,0:T(8,128)S(1)} %fusion.16), channel_id=1, replica_groups=mesh['narrow'=4,'wide'=8] {'narrow'}, dimensions={0} | all-to-all | bytes 524288 | tf_op jit(solution)/shard_map/all_to_all | solution.py:41
  23.3 0.7 copy.24
  24.1 5.8 %all-to-all-start.1 = ((f32[4,8,16,128]{3,2,0,1:T(8,128)}), f32[4,8,16,128]{3,2,0,1:T(8,128)S(1)}, u32[]{:S(2)}, u32[]{:S(2)}) async-start(f32[4,8,16,128]{3,2,0,1:T(8,128)} %copy.24), calls=%async_computation.1 | async-start | bytes 524288 | tf_op jit(solution)/shard_map/all_to_all | solution.py:40
  29.9 1.4 dynamic-slice_reduce_fusion.2
  32.6 5.8 %all-to-all-done.1 = f32[4,8,16,128]{3,2,0,1:T(8,128)S(1)} async-done(((f32[4,8,16,128]{3,2,0,1:T(8,128)}), f32[4,8,16,128]{3,2,0,1:T(8,128)S(1)}, u32[]{:S(2)}, u32[]{:S(2)}) %all-to-all-start.1) | async-done | bytes 262176 | tf_op jit(solution)/shard_map/all_to_all | solution.py:40
  38.5 0.6 multiply_reduce_fusion.2
  39.7 39.0 %all-reduce.2 = (f32[]{:T(128)}, f32[]{:T(128)}) all-reduce(f32[]{:T(128)S(6)} %add.95, f32[]{:T(128)} %multiply_reduce_fusion.2), channel_id=1, replica_groups=mesh['narrow'=4,'wide'=8] {'narrow','wide'}, use_global_device_ids=true, to_apply=%region_1.2 | all-reduce | flops 2 | bytes 16 | tf_op jit(solution)/shard_map/psum | solution.py:50
  80.1 0.7 add_maximum_fusion.2
  80.8 67.3 %all_gather.9 = f32[512,128]{1,0:T(8,128)S(1)} all-gather(f32[16,128]{1,0:T(8,128)S(1)} %add_maximum_fusion.2), channel_id=1, replica_groups=mesh['narrow'=4,'wide'=8] {'narrow','wide'}, dimensions={0}, use_global_device_ids=true | all-gather | bytes 270336 | tf_op jit(solution)/shard_map/all_gather | solution.py:56
  148.1 0.6 gather_fusion.1
  148.7 0.0 copy-start.1
  148.7 0.1 broadcast_select_fusion.1
  148.8 4.1 fusion.6
  152.9 0.6 fusion.27
  153.5 0.0 copy-done.1
  153.5 3.4 fusion.4
  156.9 0.3 fusion.14
  157.3 8.4 %all_to_all.31 = f32[4,8,16,128]{3,2,1,0:T(8,128)S(1)} all-to-all(f32[4,8,16,128]{3,2,1,0:T(8,128)S(1)} %fusion.14), channel_id=1, replica_groups=mesh['narrow'=4,'wide'=8] {'narrow'}, dimensions={0} | all-to-all | bytes 524288 | tf_op jit(solution)/shard_map/all_to_all | solution.py:41
  165.7 0.7 copy.27
  166.4 3.4 all-to-all-start.3
  169.8 0.6 dynamic-slice_reduce_fusion.1
  171.6 7.0 %all-to-all-done.3 = f32[4,8,16,128]{3,2,0,1:T(8,128)S(1)} async-done(((f32[4,8,16,128]{3,2,0,1:T(8,128)}), f32[4,8,16,128]{3,2,0,1:T(8,128)S(1)}, u32[]{:S(2)}, u32[]{:S(2)}) %all-to-all-start.3) | async-done | bytes 262176 | tf_op jit(solution)/shard_map/all_to_all | solution.py:40
  178.6 0.6 multiply_reduce_fusion.1
  179.2 38.9 %all-reduce.1 = (f32[]{:T(128)}, f32[]{:T(128)}) all-reduce(f32[]{:T(128)S(6)} %add.100, f32[]{:T(128)} %multiply_reduce_fusion.1), channel_id=1, replica_groups=mesh['narrow'=4,'wide'=8] {'narrow','wide'}, use_global_device_ids=true, to_apply=%region_8.10 | all-reduce | flops 2 | bytes 16 | tf_op jit(solution)/shard_map/psum | solution.py:50
  219.5 67.5 %all_gather.10 = f32[512,128]{1,0:T(8,128)S(1)} all-gather(f32[16,128]{1,0:T(8,128)S(1)} %add_maximum_fusion.1), channel_id=1, replica_groups=mesh['narrow'=4,'wide'=8] {'narrow','wide'}, dimensions={0}, use_global_device_ids=true | all-gather | bytes 270336 | tf_op jit(solution)/shard_map/all_gather | solution.py:56
  286.9 0.6 gather_fusion.2
  287.5 0.0 copy-start.2
  287.5 0.1 broadcast_select_fusion
  287.6 4.1 fusion.2
  291.8 0.6 fusion.29
  292.4 0.0 copy-start.4
  292.4 0.0 copy-done.2
  292.4 3.4 fusion
  295.8 0.3 fusion.12
  296.1 8.4 %all_to_all.32 = f32[4,8,16,128]{3,2,1,0:T(8,128)S(1)} all-to-all(f32[4,8,16,128]{3,2,1,0:T(8,128)S(1)} %fusion.12), channel_id=1, replica_groups=mesh['narrow'=4,'wide'=8] {'narrow'}, dimensions={0} | all-to-all | bytes 524288 | tf_op jit(solution)/shard_map/all_to_all | solution.py:41
  304.5 0.7 copy.30
  305.2 3.4 all-to-all-start.5
  308.7 0.6 dynamic-slice_reduce_fusion
  310.5 6.9 %all-to-all-done.5 = f32[4,8,16,128]{3,2,0,1:T(8,128)S(1)} async-done(((f32[4,8,16,128]{3,2,0,1:T(8,128)}), f32[4,8,16,128]{3,2,0,1:T(8,128)S(1)}, u32[]{:S(2)}, u32[]{:S(2)}) %all-to-all-start.5) | async-done | bytes 262176 | tf_op jit(solution)/shard_map/all_to_all | solution.py:40
  317.5 0.6 multiply_reduce_fusion
  318.1 38.9 %all-reduce = (f32[]{:T(128)}, f32[]{:T(128)}) all-reduce(f32[]{:T(128)S(6)} %add.106, f32[]{:T(128)} %multiply_reduce_fusion), channel_id=1, replica_groups=mesh['narrow'=4,'wide'=8] {'narrow','wide'}, use_global_device_ids=true, to_apply=%region_15.17 | all-reduce | flops 2 | bytes 16 | tf_op jit(solution)/shard_map/psum | solution.py:50
  358.2 67.3 %all_gather.11 = f32[512,128]{1,0:T(8,128)S(1)} all-gather(f32[16,128]{1,0:T(8,128)S(1)} %add_maximum_fusion), channel_id=1, replica_groups=mesh['narrow'=4,'wide'=8] {'narrow','wide'}, dimensions={0}, use_global_device_ids=true | all-gather | bytes 270336 | tf_op jit(solution)/shard_map/all_gather | solution.py:56
  425.5 0.7 copy.48
  426.2 0.0 copy-done.4
  (7 shorter events, 0.1 us)
Async XLA Ops:
  0.6 8.3 %copy-start.3 = (s32[16,128]{1,0:T(8,128)S(1)}, s32[16,128]{1,0:T(8,128)}, u32[]{:S(2)}) copy-start(s32[16,128]{1,0:T(8,128)} %param.9) | copy-start | bytes 24580
  4.7 4.9 %copy-start = (s32[16,4,128,128]{3,2,1,0:T(8,128)S(1)}, s32[16,4,128,128]{3,2,1,0:T(8,128)}, u32[]{:S(2)}) copy-start(s32[16,4,128,128]{3,2,1,0:T(8,128)} %param.8) | copy-start | bytes 12582916
  24.1 14.4 %all-to-all-start.1 = ((f32[4,8,16,128]{3,2,0,1:T(8,128)}), f32[4,8,16,128]{3,2,0,1:T(8,128)S(1)}, u32[]{:S(2)}, u32[]{:S(2)}) async-start(f32[4,8,16,128]{3,2,0,1:T(8,128)} %copy.24), calls=%async_computation.1 | async-start | bytes 524288 | tf_op jit(solution)/shard_map/all_to_all | solution.py:40
  148.7 4.8 %copy-start.1 = (s32[16,4,128,128]{3,2,1,0:T(8,128)S(1)}, s32[16,4,128,128]{3,2,1,0:T(8,128)}, u32[]{:S(2)}) copy-start(s32[16,4,128,128]{3,2,1,0:T(8,128)} %param.8) | copy-start | bytes 12582916
  166.4 12.2 %all-to-all-start.3 = ((f32[4,8,16,128]{3,2,0,1:T(8,128)}), f32[4,8,16,128]{3,2,0,1:T(8,128)S(1)}, u32[]{:S(2)}, u32[]{:S(2)}) async-start(f32[4,8,16,128]{3,2,0,1:T(8,128)} %copy.27), calls=%async_computation.3 | async-start | bytes 524288 | tf_op jit(solution)/shard_map/all_to_all | solution.py:40
  287.5 4.8 %copy-start.2 = (s32[16,4,128,128]{3,2,1,0:T(8,128)S(1)}, s32[16,4,128,128]{3,2,1,0:T(8,128)}, u32[]{:S(2)}) copy-start(s32[16,4,128,128]{3,2,1,0:T(8,128)} %param.8) | copy-start | bytes 12582916
  292.4 133.9 %copy-start.4 = (f32[16,128]{1,0:T(8,128)}, f32[16,128]{1,0:T(8,128)S(1)}, u32[]{:S(2)}) copy-start(f32[16,128]{1,0:T(8,128)S(1)} %get-tuple-element.18) | copy-start | bytes 24580
  305.2 12.2 %all-to-all-start.5 = ((f32[4,8,16,128]{3,2,0,1:T(8,128)}), f32[4,8,16,128]{3,2,0,1:T(8,128)S(1)}, u32[]{:S(2)}, u32[]{:S(2)}) async-start(f32[4,8,16,128]{3,2,0,1:T(8,128)} %copy.30), calls=%async_computation.5 | async-start | bytes 524288 | tf_op jit(solution)/shard_map/all_to_all | solution.py:40
where the time goes:
time: 427 us; the launch traced here: 426 us
  blocking collectives  346 us (81%)
  matrix products  23.5 us (6%)
  waiting for transfers between devices  19.7 us (5%)
  starting transfers between devices  12.7 us (3%)
  between operations  9.14 us (2%)
  other arithmetic  8.77 us (2%)
  local copies, waits for them, and re-layouts  6.74 us (2%)
    all_gather x3, blocking collectives, local(): mult = lax.all_gather(new_share, ('narrow', 'wide'), axis=0, tiled=True)  202 us
    psum x3, blocking collectives, local(): lax.psum((jnp.sum(slope * slope), jnp.sum(mult_share), local_soft), ('nar...  117 us
    all_to_all x3, blocking collectives, local(): lax.all_to_all(outgoing, 'narrow', split_axis=0, concat_axis=0, tiled=True)  26.8 us
    all_to_all x3, waiting for transfers between devices, local(): lax.all_to_all(lax.all_to_all(outgoing, 'narrow', split_axis=0, concat_ax...  19.7 us
    all_to_all x3, starting transfers between devices, local(): lax.all_to_all(lax.all_to_all(outgoing, 'narrow', split_axis=0, concat_ax...  12.7 us
    dot_general x3, matrix products, local(): reduced = costf - jnp.einsum('tkrc,tkr->tc', incf, u_tile, precision=hi)  12.3 us
    dot_general x3, matrix products, local(): jnp.einsum('tkrc,tc->tkr', incf, primal_mean, precision=hi)  10.2 us
  transfers between devices with their start and end apart: 3, of which 3 were waited for; matrix products, arithmetic and copies ran while one was open for 1% of the time, Pallas kernels for 0%

commit v1 on v0

--- a/solution.py
+++ b/solution.py
@@ -37,13 +37,10 @@
         )
         row_part = jnp.dot(onehot.T, part, precision=hi, preferred_element_type=jnp.float32)
         outgoing = row_part.reshape(count_narrow, count_wide, share_rows, BLK)
-        incoming = lax.all_to_all(
-            lax.all_to_all(outgoing, "narrow", split_axis=0, concat_axis=0, tiled=True),
-            "wide",
-            split_axis=1,
-            concat_axis=1,
-            tiled=True,
-        )
+        x = lax.all_to_all(outgoing, "narrow", split_axis=0, concat_axis=0, tiled=True)
+        cells = jnp.split(x, lax.axis_size("wide"), axis=1)
+        received = lax.all_to_all(jnp.stack(cells), "wide", 0, 0)
+        incoming = jnp.concatenate(received, axis=1)
         cover_share = jnp.sum(jnp.sum(incoming, axis=0), axis=0)
         mult_share = lax.dynamic_slice_in_dim(mult, share_start, share_rows, 0)
         slope = 1.0 - cover_share

time: 427 us -> 440 us (1.030)
  local copies, waits for them, and re-layouts: 6.74 us -> 19.4 us
    unnamed x12 -> x33, local copies, waits for them, and re-layouts: 1.48 us -> 14.4 us
where the time goes in v1:
time: 440 us; the launch traced here: 439 us
  blocking collectives  346 us (79%)
  matrix products  23.5 us (5%)
  waiting for transfers between devices  19.7 us (4%)
  local copies, waits for them, and re-layouts  19.4 us (4%)
  starting transfers between devices  12.7 us (3%)
  between operations  9.15 us (2%)
  other arithmetic  8.77 us (2%)
    all_gather x3, blocking collectives, local(): mult = lax.all_gather(new_share, ('narrow', 'wide'), axis=0, tiled=True)  202 us
    psum x3, blocking collectives, local(): lax.psum((jnp.sum(slope * slope), jnp.sum(mult_share), local_soft), ('nar...  117 us
    all_to_all x3, blocking collectives, local(): lax.all_to_all(outgoing, 'narrow', split_axis=0, concat_axis=0, tiled=True)  26.8 us
    all_to_all x3, waiting for transfers between devices, local(): received = lax.all_to_all(jnp.stack(cells), 'wide', 0, 0)  19.7 us
    unnamed x33, local copies, waits for them, and re-layouts  14.4 us
    all_to_all x3, starting transfers between devices, local(): received = lax.all_to_all(jnp.stack(cells), 'wide', 0, 0)  12.7 us
    dot_general x3, matrix products, local(): reduced = costf - jnp.einsum('tkrc,tkr->tc', incf, u_tile, precision=hi)  12.3 us
    dot_general x3, matrix products, local(): jnp.einsum('tkrc,tc->tkr', incf, primal_mean, precision=hi)  10.2 us
  transfers between devices with their start and end apart: 3, of which 3 were waited for; matrix products, arithmetic and copies ran while one was open for 1% of the time, Pallas kernels for 0%

profile of v1, /device:TPU:0, one launch (start us, length us, event | category | flops | bytes accessed | tf_op | source)
XLA Modules:
  0.0 438.9 jit_solution(5972429225273998544)
XLA Ops:
  0.6 0.7 compare_and_fusion
  1.3 0.7 compare_select_fusion.3
  2.0 0.8 copy.37
  3.2 1.5 gather_fusion
  4.8 4.1 fusion.10
  8.9 0.6 fusion.25
  9.6 3.4 fusion.8
  12.9 0.3 fusion.16
  13.3 10.0 %all_to_all.30 = f32[4,8,16,128]{3,2,1,0:T(8,128)S(1)} all-to-all(f32[4,8,16,128]{3,2,1,0:T(8,128)S(1)} %fusion.16), channel_id=1, replica_groups=mesh['narrow'=4,'wide'=8] {'narrow'}, dimensions={0} | all-to-all | bytes 524288 | tf_op jit(solution)/shard_map/all_to_all | solution.py:40
  23.3 0.6 constant_dynamic-update-slice_fusion.7
  24.0 0.6 constant_dynamic-update-slice_fusion.6
  24.6 0.6 constant_dynamic-update-slice_fusion.5
  25.2 0.6 constant_dynamic-update-slice_fusion.4
  25.8 0.6 constant_dynamic-update-slice_fusion.3
  26.4 0.6 constant_dynamic-update-slice_fusion.2
  27.0 0.6 constant_dynamic-update-slice_fusion.1
  27.7 0.6 constant_dynamic-update-slice_fusion
  28.3 5.8 %all-to-all-start.1 = ((f32[8,4,1,16,128]{4,3,1,2,0:T(8,128)}), f32[8,4,1,16,128]{4,3,1,2,0:T(8,128)S(1)}, u32[]{:S(2)}, u32[]{:S(2)}) async-start(f32[8,4,1,16,128]{4,3,1,2,0:T(8,128)} %constant_dynamic-update-slice_fusion), calls=%async_computation.1 | async-start | bytes 524288 | tf_op jit(solution)/shard_map/all_to_all | solution.py:42
  34.1 1.4 dynamic-slice_reduce_fusion.2
  36.8 5.8 %all-to-all-done.1 = f32[8,4,1,16,128]{4,3,1,2,0:T(8,128)S(1)} async-done(((f32[8,4,1,16,128]{4,3,1,2,0:T(8,128)}), f32[8,4,1,16,128]{4,3,1,2,0:T(8,128)S(1)}, u32[]{:S(2)}, u32[]{:S(2)}) %all-to-all-start.1) | async-done | bytes 262176 | tf_op jit(solution)/shard_map/all_to_all | solution.py:42
  42.7 0.6 multiply_reduce_fusion.2
  44.0 39.0 %all-reduce.2 = (f32[]{:T(128)}, f32[]{:T(128)}) all-reduce(f32[]{:T(128)S(6)} %add.95, f32[]{:T(128)} %multiply_reduce_fusion.2), channel_id=1, replica_groups=mesh['narrow'=4,'wide'=8] {'narrow','wide'}, use_global_device_ids=true, to_apply=%region_1.2 | all-reduce | flops 2 | bytes 16 | tf_op jit(solution)/shard_map/psum | solution.py:47
  84.3 0.7 add_maximum_fusion.2
  85.1 67.3 %all_gather.9 = f32[512,128]{1,0:T(8,128)S(1)} all-gather(f32[16,128]{1,0:T(8,128)S(1)} %add_maximum_fusion.2), channel_id=1, replica_groups=mesh['narrow'=4,'wide'=8] {'narrow','wide'}, dimensions={0}, use_global_device_ids=true | all-gather | bytes 270336 | tf_op jit(solution)/shard_map/all_gather | solution.py:53
  152.3 0.6 gather_fusion.1
  153.0 4.1 fusion.6
  157.1 0.6 fusion.27
  157.7 3.4 fusion.4
  161.5 8.4 %all_to_all.31 = f32[4,8,16,128]{3,2,1,0:T(8,128)S(1)} all-to-all(f32[4,8,16,128]{3,2,1,0:T(8,128)S(1)} %fusion.14), channel_id=1, replica_groups=mesh['narrow'=4,'wide'=8] {'narrow'}, dimensions={0} | all-to-all | bytes 524288 | tf_op jit(solution)/shard_map/all_to_all | solution.py:40
  169.9 0.6 constant_dynamic-update-slice_fusion.15
  170.5 0.6 constant_dynamic-update-slice_fusion.14
  171.1 0.6 constant_dynamic-update-slice_fusion.13
  171.7 0.6 constant_dynamic-update-slice_fusion.12
  172.3 0.6 constant_dynamic-update-slice_fusion.11
  173.0 0.6 constant_dynamic-update-slice_fusion.10
  173.6 0.6 constant_dynamic-update-slice_fusion.9
  174.2 0.6 constant_dynamic-update-slice_fusion.8
  174.8 3.4 all-to-all-start.3
  178.2 0.6 dynamic-slice_reduce_fusion.1
  180.1 7.0 %all-to-all-done.3 = f32[8,4,1,16,128]{4,3,1,2,0:T(8,128)S(1)} async-done(((f32[8,4,1,16,128]{4,3,1,2,0:T(8,128)}), f32[8,4,1,16,128]{4,3,1,2,0:T(8,128)S(1)}, u32[]{:S(2)}, u32[]{:S(2)}) %all-to-all-start.3) | async-done | bytes 262176 | tf_op jit(solution)/shard_map/all_to_all | solution.py:42
  187.0 0.6 multiply_reduce_fusion.1
  187.6 38.9 %all-reduce.1 = (f32[]{:T(128)}, f32[]{:T(128)}) all-reduce(f32[]{:T(128)S(6)} %add.100, f32[]{:T(128)} %multiply_reduce_fusion.1), channel_id=1, replica_groups=mesh['narrow'=4,'wide'=8] {'narrow','wide'}, use_global_device_ids=true, to_apply=%region_8.10 | all-reduce | flops 2 | bytes 16 | tf_op jit(solution)/shard_map/psum | solution.py:47
  227.9 67.5 %all_gather.10 = f32[512,128]{1,0:T(8,128)S(1)} all-gather(f32[16,128]{1,0:T(8,128)S(1)} %add_maximum_fusion.1), channel_id=1, replica_groups=mesh['narrow'=4,'wide'=8] {'narrow','wide'}, dimensions={0}, use_global_device_ids=true | all-gather | bytes 270336 | tf_op jit(solution)/shard_map/all_gather | solution.py:53
  295.4 0.6 gather_fusion.2
  296.1 4.1 fusion.2
  300.2 0.6 fusion.29
  300.8 3.4 fusion
  304.2 0.3 fusion.12
  304.5 8.4 %all_to_all.32 = f32[4,8,16,128]{3,2,1,0:T(8,128)S(1)} all-to-all(f32[4,8,16,128]{3,2,1,0:T(8,128)S(1)} %fusion.12), channel_id=1, replica_groups=mesh['narrow'=4,'wide'=8] {'narrow'}, dimensions={0} | all-to-all | bytes 524288 | tf_op jit(solution)/shard_map/all_to_all | solution.py:40
  312.9 0.6 constant_dynamic-update-slice_fusion.23
  313.6 0.6 constant_dynamic-update-slice_fusion.22
  314.2 0.6 constant_dynamic-update-slice_fusion.21
  314.8 0.6 constant_dynamic-update-slice_fusion.20
  315.4 0.6 constant_dynamic-update-slice_fusion.19
  316.0 0.6 constant_dynamic-update-slice_fusion.18
  316.6 0.6 constant_dynamic-update-slice_fusion.17
  317.3 0.6 constant_dynamic-update-slice_fusion.16
  317.9 3.4 all-to-all-start.5
  321.3 0.6 dynamic-slice_reduce_fusion
  323.1 6.9 %all-to-all-done.5 = f32[8,4,1,16,128]{4,3,1,2,0:T(8,128)S(1)} async-done(((f32[8,4,1,16,128]{4,3,1,2,0:T(8,128)}), f32[8,4,1,16,128]{4,3,1,2,0:T(8,128)S(1)}, u32[]{:S(2)}, u32[]{:S(2)}) %all-to-all-start.5) | async-done | bytes 262176 | tf_op jit(solution)/shard_map/all_to_all | solution.py:42
  330.1 0.6 multiply_reduce_fusion
  330.7 38.9 %all-reduce = (f32[]{:T(128)}, f32[]{:T(128)}) all-reduce(f32[]{:T(128)S(6)} %add.106, f32[]{:T(128)} %multiply_reduce_fusion), channel_id=1, replica_groups=mesh['narrow'=4,'wide'=8] {'narrow','wide'}, use_global_device_ids=true, to_apply=%region_15.17 | all-reduce | flops 2 | bytes 16 | tf_op jit(solution)/shard_map/psum | solution.py:47
  370.9 67.3 %all_gather.11 = f32[512,128]{1,0:T(8,128)S(1)} all-gather(f32[16,128]{1,0:T(8,128)S(1)} %add_maximum_fusion), channel_id=1, replica_groups=mesh['narrow'=4,'wide'=8] {'narrow','wide'}, dimensions={0}, use_global_device_ids=true | all-gather | bytes 270336 | tf_op jit(solution)/shard_map/all_gather | solution.py:53
  438.2 0.7 copy.122
  (25 shorter events, 1.1 us)
Async XLA Ops:
  0.6 8.3 %copy-start.3 = (s32[16,128]{1,0:T(8,128)S(1)}, s32[16,128]{1,0:T(8,128)}, u32[]{:S(2)}) copy-start(s32[16,128]{1,0:T(8,128)} %param.9) | copy-start | bytes 24580
  4.7 4.9 %copy-start = (s32[16,4,128,128]{3,2,1,0:T(8,128)S(1)}, s32[16,4,128,128]{3,2,1,0:T(8,128)}, u32[]{:S(2)}) copy-start(s32[16,4,128,128]{3,2,1,0:T(8,128)} %param.8) | copy-start | bytes 12582916
  28.3 14.4 %all-to-all-start.1 = ((f32[8,4,1,16,128]{4,3,1,2,0:T(8,128)}), f32[8,4,1,16,128]{4,3,1,2,0:T(8,128)S(1)}, u32[]{:S(2)}, u32[]{:S(2)}) async-start(f32[8,4,1,16,128]{4,3,1,2,0:T(8,128)} %constant_dynamic-update-slice_fusion), calls=%async_computation.1 | async-start | bytes 524288 | tf_op jit(solution)/shard_map/all_to_all | solution.py:42
  152.9 4.8 %copy-start.1 = (s32[16,4,128,128]{3,2,1,0:T(8,128)S(1)}, s32[16,4,128,128]{3,2,1,0:T(8,128)}, u32[]{:S(2)}) copy-start(s32[16,4,128,128]{3,2,1,0:T(8,128)} %param.8) | copy-start | bytes 12582916
  174.8 12.2 %all-to-all-start.3 = ((f32[8,4,1,16,128]{4,3,1,2,0:T(8,128)}), f32[8,4,1,16,128]{4,3,1,2,0:T(8,128)S(1)}, u32[]{:S(2)}, u32[]{:S(2)}) async-start(f32[8,4,1,16,128]{4,3,1,2,0:T(8,128)} %constant_dynamic-update-slice_fusion.8), calls=%async_computation.3 | async-start | bytes 524288 | tf_op jit(solution)/shard_map/all_to_all | solution.py:42
  296.0 4.8 %copy-start.2 = (s32[16,4,128,128]{3,2,1,0:T(8,128)S(1)}, s32[16,4,128,128]{3,2,1,0:T(8,128)}, u32[]{:S(2)}) copy-start(s32[16,4,128,128]{3,2,1,0:T(8,128)} %param.8) | copy-start | bytes 12582916
  300.8 138.1 %copy-start.4 = (f32[16,128]{1,0:T(8,128)}, f32[16,128]{1,0:T(8,128)S(1)}, u32[]{:S(2)}) copy-start(f32[16,128]{1,0:T(8,128)S(1)} %get-tuple-element.18) | copy-start | bytes 24580
  317.9 12.2 %all-to-all-start.5 = ((f32[8,4,1,16,128]{4,3,1,2,0:T(8,128)}), f32[8,4,1,16,128]{4,3,1,2,0:T(8,128)S(1)}, u32[]{:S(2)}, u32[]{:S(2)}) async-start(f32[8,4,1,16,128]{4,3,1,2,0:T(8,128)} %constant_dynamic-update-slice_fusion.16), calls=%async_computation.5 | async-start | bytes 524288 | tf_op jit(solution)/shard_map/all_to_all | solution.py:42
